TPU v7x, 256 devices: a whole 4x4x8 slice. The times are simulated.
256 devices in a mesh: seq: 32 (over y, x, core), head: 8 (over z).
Axes of the slice: x: 4, y: 4, z: 8, core: 2. Of those that a mesh axis runs over, the one named last changes fastest.
Arguments:
- old_cache: bfloat16 [2048, 8, 128, 128], P(('seq', 'head')), may hold values from -9 to 9
- page_dest: int32 [2048], P(('seq', 'head')), may hold values from 0 to 2047, as said below
- seq_pages: int32 [64], replicated, may hold values from 1 to 128, 2048 in all
- last_fill: int32 [64], replicated, may hold values from 1 to 128
- queries: bfloat16 [64, 8, 512], P(None, 'head'), may hold values from -16 to 16
Outputs:
- new_cache: bfloat16 [2048, 8, 128, 128], P('seq', 'head')
- attended: bfloat16 [64, 8, 512], P('seq', 'head')
Inputs may be any that keep to these rules, and one draw needn't show every extreme that they name: page_dest is a permutation of the page numbers. The 64 old pages p with the same p // 64 go to exactly 16 distinct new owners page_dest[p] // 64, exactly 4 pages to each; every new owner receives 64 pages.
All inputs are finite; a program needn't handle non-finite values.
Results may differ from a plain program's by a relative error of at most 0.004.
Values may be sent and summed in bfloat16 or wider, within the bound.
A program may use at most 64 MiB of HBM per device.

v0:
```python
import jax
import jax.numpy as jnp
from jax import lax
from jax.sharding import PartitionSpec as P

NEG_FILL = -1e30


def from_everyone(shard, axis):
    copies = jnp.broadcast_to(shard, (lax.axis_size(axis), *shard.shape))
    return lax.all_to_all(copies, axis, split_axis=0, concat_axis=0, tiled=True)


def over_copies(shard, axis):
    return from_everyone(shard, axis).max(axis=0)


def split_up(shard, dim, length):
    dims = shard.shape
    pieces = shard.reshape(*dims[:dim], length, dims[dim] // length, *dims[dim + 1 :])
    return jnp.moveaxis(pieces, dim, 0)


def summed_on_arrival(shard, axis, dim):
    length = lax.axis_size(axis)
    pieces = lax.all_to_all(split_up(shard, dim, length), axis, 0, 0, tiled=True)
    return jnp.sum(pieces, axis=0)


def side_by_side(arrays, axis, dim, along):
    widths = [a.shape[along] for a in arrays]
    both = jnp.concatenate(arrays, axis=along)
    filled = summed_on_arrival(both, axis, dim)
    return tuple(jnp.split(filled, [sum(widths[:k]) for k in range(1, len(widths))], axis=along))


def page_layout(index_new, seq_pages, last_fill, seq_total, page_len, page_count, seq_peers):
    position = index_new % page_count * seq_peers + index_new // page_count
    seq_ends = jnp.cumsum(seq_pages)
    page_owner = jnp.sum((position[:, None] >= seq_ends[None, :]).astype(jnp.int32), axis=1)
    member = page_owner[:, None] == jnp.arange(seq_total, dtype=jnp.int32)[None, :]
    owner_end = jnp.sum(jnp.where(member, seq_ends[None, :], 0), axis=1)
    owner_fill = jnp.sum(jnp.where(member, last_fill[None, :], 0), axis=1)
    page_fill = jnp.where(position == owner_end - 1, owner_fill, page_len)
    token_live = jnp.arange(page_len, dtype=jnp.int32)[None, :] < page_fill[:, None]
    return (member, token_live)


def local_scores(page_block, member, token_live, queries):
    page_count, head_count, page_len, double = page_block.shape
    head_width = double // 2
    group_size = queries.shape[2] // head_width
    page_query = jnp.dot(
        member.astype(jnp.bfloat16),
        queries.reshape(queries.shape[0], -1),
        preferred_element_type=jnp.float32,
    ).astype(jnp.bfloat16)
    page_query = page_query.reshape(page_count, head_count, group_size, head_width)
    scores = jnp.einsum(
        "pkgd,pktd->pkgt",
        page_query,
        page_block[..., :head_width],
        preferred_element_type=jnp.float32,
    ) * head_width ** (-0.5)
    scores = jnp.where(token_live[:, None, None, :], scores, NEG_FILL)
    page_max = jnp.max(scores, axis=3)
    seq_local = jnp.max(jnp.where(member.T[:, :, None, None], page_max[None], NEG_FILL), axis=1)
    return (scores, seq_local.reshape(queries.shape[0], -1))


def partial_sums(page_block, member, token_live, scores, seq_max):
    page_count = page_block.shape[0]
    head_width = page_block.shape[3] // 2
    member_float = member.astype(jnp.float32)
    owner_max = jnp.dot(member_float, seq_max, precision=lax.Precision.HIGHEST).reshape(
        scores.shape[:3]
    )
    weights = jnp.where(
        token_live[:, None, None, :], jnp.exp(scores - owner_max[..., None]), 0.0
    ).astype(jnp.bfloat16)
    page_total = jnp.sum(weights.astype(jnp.float32), axis=3)
    page_sum = jnp.einsum(
        "pkgt,pktd->pkgd", weights, page_block[..., head_width:], preferred_element_type=jnp.float32
    )
    totals = jnp.dot(
        member_float.T, page_total.reshape(page_count, -1), precision=lax.Precision.HIGHEST
    )
    weighted = jnp.dot(
        member_float.T, page_sum.reshape(page_count, -1), precision=lax.Precision.HIGHEST
    )
    return (weighted, totals)


def route_pages(page_block, index_new, seq_peers):
    page_count = page_block.shape[0]
    slot_cap = page_count // min(seq_peers, 16)
    target = index_new // page_count
    slot_new = index_new % page_count
    order_ids = jnp.arange(page_count, dtype=jnp.int32)
    earlier = (target[None, :] == target[:, None]) & (order_ids[None, :] < order_ids[:, None])
    position = target * slot_cap + jnp.sum(earlier.astype(jnp.int32), axis=1)
    matches = position[None, :] == jnp.arange(seq_peers * slot_cap, dtype=jnp.int32)[:, None]
    source = jnp.sum(jnp.where(matches, order_ids[None, :], 0), axis=1)
    filled = jnp.any(matches, axis=1)
    outgoing = jnp.where(
        filled[:, None, None, None],
        jnp.take(page_block, source, axis=0),
        jnp.zeros((), jnp.bfloat16),
    )
    labels = jnp.where(filled, jnp.take(slot_new, source), -1).astype(jnp.int32)
    return (
        outgoing.reshape((seq_peers, slot_cap) + page_block.shape[1:]),
        labels.reshape(seq_peers, slot_cap),
    )


def move_pages(outgoing, labels, page_count):
    incoming, tag_list = (
        lax.all_to_all(outgoing, "seq", split_axis=0, concat_axis=0, tiled=True),
        lax.all_to_all(labels, "seq", split_axis=0, concat_axis=0, tiled=True),
    )
    flat_pages = incoming.reshape((-1,) + incoming.shape[2:])
    flat_labels = tag_list.reshape(-1)
    slot_ids = jnp.arange(flat_labels.shape[0], dtype=jnp.int32)
    matches = flat_labels[None, :] == jnp.arange(page_count, dtype=jnp.int32)[:, None]
    anchor = jnp.sum(jnp.where(matches, slot_ids[None, :], 0), axis=1)
    return jnp.take(flat_pages, anchor, axis=0)


def per_device(old_cache, page_dest, seq_pages, last_fill, queries):
    spread = jnp.broadcast_to(page_dest[:, None], (page_dest.shape[0], old_cache.shape[1]))
    regrouped, spread_back = (
        lax.all_to_all(old_cache, "head", split_axis=1, concat_axis=0, tiled=True),
        lax.all_to_all(spread, "head", split_axis=1, concat_axis=0, tiled=True),
    )
    index_old = spread_back[:, 0]
    page_count = regrouped.shape[0]
    page_len = regrouped.shape[2]
    head_count = regrouped.shape[1]
    head_width = regrouped.shape[3] // 2
    seq_peers = lax.axis_size("seq")
    seq_total = queries.shape[0]
    outgoing, labels = route_pages(regrouped, index_old, seq_peers)
    member, token_live = page_layout(
        index_old, seq_pages, last_fill, seq_total, page_len, page_count, seq_peers
    )
    scores, seq_local = local_scores(regrouped, member, token_live, queries)
    new_cache = move_pages(outgoing, labels, page_count)
    seq_max = over_copies(seq_local, "seq")
    weighted, totals = partial_sums(regrouped, member, token_live, scores, seq_max)
    local_seqs = seq_total // seq_peers
    weighted, totals = side_by_side((weighted, totals), "seq", 0, 1)
    result = weighted.reshape(local_seqs, -1, head_width) / totals[:, :, None]
    attended = result.reshape(local_seqs, head_count, -1).astype(jnp.bfloat16)
    return (new_cache, attended)


def solution(mesh):
    in_specs = (
        P(("seq", "head"), None, None, None),
        P(("seq", "head")),
        P(),
        P(),
        P(None, "head", None),
    )
    out_specs = (P("seq", "head", None, None), P("seq", "head", None))
    return jax.shard_map(
        per_device, mesh=mesh, in_specs=in_specs, out_specs=out_specs, check_vma=False
    )
```

profile of v0, /device:TPU:1, one launch (start us, length us, event | category | flops | bytes accessed | tf_op | source)
XLA Modules:
  0.0 177.8 jit_solution(13307670082451872531)
XLA Ops:
  0.6 1.3 broadcast_in_dim.158
  1.9 9.0 %all-to-all-start = ((s32[8,8,1]{0,2,1:T(1,128)}), s32[8,8,1]{0,2,1:T(1,128)S(1)}, u32[]{:S(2)}, u32[]{:S(2)}) async-start(s32[8,8,1]{0,2,1:T(1,128)} %broadcast_in_dim.158), calls=%async_computation | async-start | bytes 8192 | tf_op jit(solution)/shard_map/all_to_all | solution.py:134
  10.9 3.2 %copy.39 = bf16[8,8,128,128]{3,2,0,1:T(8,128)(2,1)} copy(bf16[8,8,128,128]{3,2,1,0:T(8,128)(2,1)} %param.5) | data formatting | bytes 4194304 | tf_op args[0]
  14.1 3.4 %all-to-all-done = s32[8,8,1]{0,2,1:T(1,128)S(1)} async-done(((s32[8,8,1]{0,2,1:T(1,128)}), s32[8,8,1]{0,2,1:T(1,128)S(1)}, u32[]{:S(2)}, u32[]{:S(2)}) %all-to-all-start) | async-done | bytes 288 | tf_op jit(solution)/shard_map/all_to_all | solution.py:134
  17.5 3.6 %all-to-all-start.2 = ((bf16[8,8,128,128]{3,2,0,1:T(8,128)(2,1)}), bf16[8,8,128,128]{3,2,0,1:T(8,128)(2,1)S(1)}, u32[]{:S(2)}, u32[]{:S(2)}) async-start(bf16[8,8,128,128]{3,2,0,1:T(8,128)(2,1)} %copy.39), calls=%async_computation.2 | async-start | bytes 4194304 | tf_op jit(solution)/shard_map/all_to_all | solution.py:133
  21.1 0.1 copy.41
  21.3 0.1 reduce.7
  21.5 0.2 convert_reduce_fusion.1
  21.8 0.1 reduce_sum.85
  21.9 0.1 reduce_sum.82
  22.1 0.1 reduce_or.12
  22.3 1.2 gather_fusion
  23.6 0.2 convolution_convert_fusion
  23.8 0.1 reshape.394
  24.0 0.2 select_reduce_fusion.2
  24.3 0.6 select_select_fusion.1
  24.9 47.8 %all-to-all-done.2 = bf16[8,8,128,128]{3,2,0,1:T(8,128)(2,1)S(1)} async-done(((bf16[8,8,128,128]{3,2,0,1:T(8,128)(2,1)}), bf16[8,8,128,128]{3,2,0,1:T(8,128)(2,1)S(1)}, u32[]{:S(2)}, u32[]{:S(2)}) %all-to-all-start.2) | async-done | bytes 2097184 | tf_op jit(solution)/shard_map/all_to_all | solution.py:133
  72.7 2.6 %copy.42 = bf16[8,8,1,128,128]{3,4,1,0,2:T(8,128)(2,1)} copy(bf16[8,8,1,128,128]{4,3,1,0,2:T(8,128)(2,1)S(1)} %bitcast.45) | data formatting | bytes 4194304 | tf_op jit(solution)/shard_map/all_to_all | solution.py:133
  75.3 1.7 fusion.16
  77.0 0.2 select_reduce_fusion
  77.3 0.8 reshape.445
  78.0 7.6 %all-to-all-start.4 = ((f32[32,1,512]{2,1,0:T(1,128)}), f32[32,1,512]{2,1,0:T(1,128)S(1)}, u32[]{:S(2)}, u32[]{:S(2)}) async-start(f32[32,1,512]{2,1,0:T(1,128)} %reshape.445), calls=%async_computation.4 | async-start | bytes 131072 | tf_op jit(solution)/shard_map/all_to_all | solution.py:11
  85.7 0.1 broadcast_in_dim.166
  85.8 3.0 %gather_fusion.1 = bf16[128,128,128]{2,1,0:T(8,128)(2,1)} fusion(bf16[64,128,128]{2,1,0:T(8,128)(2,1)S(1)} %bitcast.46, s32[1024]{0:T(1024)S(1)} %pad_clamp_fusion.1), kind=kCustom, calls=%fused_computation.1 | custom fusion | bytes 8389120 | tf_op jit(solution)/shard_map/jit(_take)/gather | solution.py:107
  88.8 4.2 %all-to-all-done.4 = f32[32,1,512]{2,1,0:T(1,128)S(1)} async-done(((f32[32,1,512]{2,1,0:T(1,128)}), f32[32,1,512]{2,1,0:T(1,128)S(1)}, u32[]{:S(2)}, u32[]{:S(2)}) %all-to-all-start.4) | async-done | bytes 65568 | tf_op jit(solution)/shard_map/all_to_all | solution.py:11
  93.0 3.8 %all-to-all-start.1 = ((s32[32,1,4]{2,1,0:T(1,128)}), s32[32,1,4]{2,1,0:T(1,128)S(1)}, u32[]{:S(2)}, u32[]{:S(2)}) async-start(s32[32,1,4]{2,1,0:T(1,128)} %bitcast.3), calls=%async_computation.1 | async-start | bytes 32768 | tf_op jit(solution)/shard_map/all_to_all | solution.py:120
  96.8 0.5 broadcast.439
  97.3 0.8 reduce.14
  98.3 0.2 fusion.5
  98.5 1.9 %fusion.1 = f32[64,8,64]{2,1,0:T(8,128)S(1)} fusion(bf16[64,1,128,128]{2,3,0,1:T(8,128)(2,1)} %bitcast.49, f32[64,8,128]{2,1,0:T(8,128)S(1)} %get-tuple-element.8, f32[64,8]{1,0:T(8,128)S(1)} %fusion.5, pred[64,128]{1,0:T(8,128)(4,1)S(1)} %iota_compare_fusion.1), kind=kOutput, calls=%fused_computation.9 | convolution fusion | flops 8585216 | bytes 1452032 | tf_op jit(solution)/shard_map/pkgt,pktd->pkgd/dot_general | solution.py:82
  100.4 0.2 convert_reduce_fusion
  100.6 0.1 reshape.397
  100.8 0.3 fusion.4
  101.1 0.3 fusion.3
  101.4 0.8 reshape.398
  102.2 1.7 all-to-all-done.1
  103.9 5.8 %all-to-all-start.5 = ((f32[32,2,520]{2,1,0:T(2,128)}), f32[32,2,520]{2,1,0:T(2,128)S(1)}, u32[]{:S(2)}, u32[]{:S(2)}) async-start(f32[32,2,520]{2,1,0:T(2,128)} %reshape.398), calls=%async_computation.5 | async-start | bytes 327680 | tf_op jit(solution)/shard_map/all_to_all | solution.py:26
  109.7 3.9 %select_select_fusion = bf16[32,4,1,128,128]{4,3,1,2,0:T(8,128)(2,1)} fusion(bf16[32,4,1,128,128]{4,3,1,2,0:T(8,128)(2,1)} %bitcast.47, pred[32,4]{1,0:T(8,128)(4,1)S(1)} %compare_and_fusion, pred[32,4]{1,0:T(8,128)(4,1)S(1)} %broadcast_in_dim.166), kind=kLoop, calls=%fused_computation.3 | loop fusion | flops 4194304 | bytes 8388864 | tf_op jit(solution)/shard_map/jit(_where)/select_n | solution.py:105
  113.6 4.0 %all-to-all-done.5 = f32[32,2,520]{2,1,0:T(2,128)S(1)} async-done(((f32[32,2,520]{2,1,0:T(2,128)}), f32[32,2,520]{2,1,0:T(2,128)S(1)}, u32[]{:S(2)}, u32[]{:S(2)}) %all-to-all-start.5) | async-done | bytes 133152 | tf_op jit(solution)/shard_map/all_to_all | solution.py:26
  117.6 4.7 %all-to-all-start.3 = ((bf16[32,4,1,128,128]{4,3,1,2,0:T(8,128)(2,1)}), bf16[32,4,1,128,128]{4,3,1,2,0:T(8,128)(2,1)}, u32[]{:S(2)}, u32[]{:S(2)}) async-start(bf16[32,4,1,128,128]{4,3,1,2,0:T(8,128)(2,1)} %select_select_fusion), calls=%async_computation.3 | async-start | bytes 8388608 | tf_op jit(solution)/shard_map/all_to_all | solution.py:119
  122.3 0.5 broadcast.435
  122.8 0.7 reduce.13
  123.5 0.1 eq.77
  123.6 0.1 select_reduce_fusion.3
  124.0 0.6 fusion.13
  124.6 48.4 %all-to-all-done.3 = bf16[32,4,1,128,128]{4,3,1,2,0:T(8,128)(2,1)} async-done(((bf16[32,4,1,128,128]{4,3,1,2,0:T(8,128)(2,1)}), bf16[32,4,1,128,128]{4,3,1,2,0:T(8,128)(2,1)}, u32[]{:S(2)}, u32[]{:S(2)}) %all-to-all-start.3) | async-done | bytes 4194336 | tf_op jit(solution)/shard_map/all_to_all | solution.py:119
  173.0 3.1 %gather_fusion.2 = bf16[64,128,128]{2,1,0:T(8,128)(2,1)S(1)} fusion(bf16[128,128,128]{2,1,0:T(8,128)(2,1)} %bitcast.9, s32[1024]{0:T(1024)S(1)} %pad_clamp_fusion), kind=kCustom, calls=%fused_computation.2 | custom fusion | bytes 4194560 | tf_op jit(solution)/shard_map/jit(_take)/gather | solution.py:127
  176.2 1.6 bitcast_select_fusion
  (33 shorter events, 1.1 us)
Async XLA Ops:
  0.6 23.0 %copy-start = (bf16[64,1,512]{2,0,1:T(8,128)(2,1)S(1)}, bf16[64,1,512]{2,0,1:T(8,128)(2,1)}, u32[]{:S(2)}) copy-start(bf16[64,1,512]{2,0,1:T(8,128)(2,1)} %param.9) | copy-start | bytes 196612
  1.9 15.6 %all-to-all-start = ((s32[8,8,1]{0,2,1:T(1,128)}), s32[8,8,1]{0,2,1:T(1,128)S(1)}, u32[]{:S(2)}, u32[]{:S(2)}) async-start(s32[8,8,1]{0,2,1:T(1,128)} %broadcast_in_dim.158), calls=%async_computation | async-start | bytes 8192 | tf_op jit(solution)/shard_map/all_to_all | solution.py:134
  14.1 7.0 %copy-start.1 = (s32[64]{0:T(128)S(1)}, s32[64]{0:T(128)}, u32[]{:S(2)}) copy-start(s32[64]{0:T(128)} %param.7) | copy-start | bytes 772
  14.1 9.9 %copy-start.2 = (s32[64]{0:T(128)S(1)}, s32[64]{0:T(128)}, u32[]{:S(2)}) copy-start(s32[64]{0:T(128)} %param.8) | copy-start | bytes 772
  17.5 55.2 %all-to-all-start.2 = ((bf16[8,8,128,128]{3,2,0,1:T(8,128)(2,1)}), bf16[8,8,128,128]{3,2,0,1:T(8,128)(2,1)S(1)}, u32[]{:S(2)}, u32[]{:S(2)}) async-start(bf16[8,8,128,128]{3,2,0,1:T(8,128)(2,1)} %copy.39), calls=%async_computation.2 | async-start | bytes 4194304 | tf_op jit(solution)/shard_map/all_to_all | solution.py:133
  78.0 15.0 %all-to-all-start.4 = ((f32[32,1,512]{2,1,0:T(1,128)}), f32[32,1,512]{2,1,0:T(1,128)S(1)}, u32[]{:S(2)}, u32[]{:S(2)}) async-start(f32[32,1,512]{2,1,0:T(1,128)} %reshape.445), calls=%async_computation.4 | async-start | bytes 131072 | tf_op jit(solution)/shard_map/all_to_all | solution.py:11
  93.0 10.9 %all-to-all-start.1 = ((s32[32,1,4]{2,1,0:T(1,128)}), s32[32,1,4]{2,1,0:T(1,128)S(1)}, u32[]{:S(2)}, u32[]{:S(2)}) async-start(s32[32,1,4]{2,1,0:T(1,128)} %bitcast.3), calls=%async_computation.1 | async-start | bytes 32768 | tf_op jit(solution)/shard_map/all_to_all | solution.py:120
  103.9 13.7 %all-to-all-start.5 = ((f32[32,2,520]{2,1,0:T(2,128)}), f32[32,2,520]{2,1,0:T(2,128)S(1)}, u32[]{:S(2)}, u32[]{:S(2)}) async-start(f32[32,2,520]{2,1,0:T(2,128)} %reshape.398), calls=%async_computation.5 | async-start | bytes 327680 | tf_op jit(solution)/shard_map/all_to_all | solution.py:26
  117.6 55.5 %all-to-all-start.3 = ((bf16[32,4,1,128,128]{4,3,1,2,0:T(8,128)(2,1)}), bf16[32,4,1,128,128]{4,3,1,2,0:T(8,128)(2,1)}, u32[]{:S(2)}, u32[]{:S(2)}) async-start(bf16[32,4,1,128,128]{4,3,1,2,0:T(8,128)(2,1)} %select_select_fusion), calls=%async_computation.3 | async-start | bytes 8388608 | tf_op jit(solution)/shard_map/all_to_all | solution.py:119
where the time goes:
time: 179 us; the launch traced here: 178 us
  waiting for transfers between devices  110 us (61%)
  starting transfers between devices  34.6 us (19%)
  local copies, waits for them, and re-layouts  18.4 us (10%)
  other arithmetic  9.7 us (5%)
  matrix products  4.63 us (3%)
    all_to_all x1, waiting for transfers between devices, move_pages(): lax.all_to_all(outgoing, 'seq', split_axis=0, concat_axis=0, tiled=True)  48.4 us
    all_to_all x1, waiting for transfers between devices, per_device(): lax.all_to_all(old_cache, 'head', split_axis=1, concat_axis=0, tiled=True)  47.8 us
    all_to_all x1, starting transfers between devices, per_device(): lax.all_to_all(spread, 'head', split_axis=1, concat_axis=0, tiled=True)  9 us
    all_to_all x1, starting transfers between devices, from_everyone(): return lax.all_to_all(copies, axis, split_axis=0, concat_axis=0, tiled=True)  7.63 us
    all_to_all x1, starting transfers between devices, summed_on_arrival(): lax.all_to_all(split_up(shard, dim, length), axis, 0, 0, tiled=True)  5.77 us
    all_to_all x1, starting transfers between devices, move_pages(): lax.all_to_all(outgoing, 'seq', split_axis=0, concat_axis=0, tiled=True)  4.75 us
    all_to_all x1, waiting for transfers between devices, from_everyone(): return lax.all_to_all(copies, axis, split_axis=0, concat_axis=0, tiled=True)  4.17 us
    unnamed x10, local copies, waits for them, and re-layouts  4.04 us
  transfers between devices with their start and end apart: 6, of which 6 were waited for; matrix products, arithmetic and copies ran while one was open for 12% of the time, Pallas kernels for 0%

commit v1 on v0

v1 whole, which is shorter than its diff:
```python
import functools

import jax
import jax.numpy as jnp
from jax import lax
from jax.experimental import pallas as pl
from jax.experimental.pallas import tpu as pltpu
from jax.sharding import PartitionSpec as P

NEG_FILL = -1e30
CHUNKS = 8
TOK = 16
LANES = 128
MESH = pl.DeviceIdType.MESH

CHIP_ORDER = (
    (1, 2), (2, 3), (3, 2), (2, 1), (1, 1), (3, 3), (0, 2), (2, 0),
    (1, 3), (3, 1), (2, 2), (0, 1), (1, 0), (0, 3), (3, 0),
)
PEERS = tuple((y, x, c) for c in (0, 1) for y, x in CHIP_ORDER) + ((0, 0, 1),)
HEAD_ORDER = (4, 3, 5, 2, 6, 1, 7)


def iota(shape, dim):
    return lax.broadcasted_iota(jnp.int32, shape, dim)


def seq_peer(seq, offset):
    dy, dx, dc = offset
    y, x, c = seq // 8, (seq // 2) % 4, seq % 2
    return ((y + dy) % 4) * 8 + ((x + dx) % 4) * 2 + (c + dc) % 2


def remote(src, dst, send_sem, recv_sem, device):
    return pltpu.make_async_remote_copy(
        src_ref=src, dst_ref=dst, send_sem=send_sem, recv_sem=recv_sem,
        device_id=device, device_id_type=MESH,
    )


def wait_bytes(ref, sem):
    pltpu.make_async_copy(ref, ref, sem).wait()


def kernel(
    old_hbm, dest_s, meta_v, q3, out_v, att_v,
    old_v, dst_v, lab_out, lab_in, tab_v, tab_s, tab2_v, tab2_s,
    fill_v, memb_v, sc_v, m_v, o_v, c_v, rj_v, r4_v, rb_v, regs, outgs, incs,
    zs, zr, xs, xr, ds, dr, ls, lr, ps, pr, ld, tsem, t2sem,
):
    h = lax.axis_index("head")
    s = lax.axis_index("seq")
    n_head, n_seq = 8, 32

    load = pltpu.make_async_copy(old_hbm, old_v, ld)
    load.start()
    bar = pltpu.get_barrier_semaphore()

    @pl.loop(1, n_head)
    def _(d):
        pl.semaphore_signal(bar, inc=1, device_id={"head": (h + d) % n_head}, device_id_type=MESH)

    @pl.loop(1, n_seq)
    def _(d):
        pl.semaphore_signal(bar, inc=1, device_id={"seq": (s + d) % n_seq}, device_id_type=MESH)

    own = pl.ds(pl.multiple_of(h * 8, 8), 8)
    row8 = iota((8, LANES), 0)
    mine = jnp.zeros((8, LANES), jnp.int32)
    for i in range(8):
        mine = jnp.where(row8 == i, dest_s[i], mine)
    dst_v[own, :] = mine

    sub, lane = iota((LANES, LANES), 0), iota((LANES, LANES), 1)
    pages_row = meta_v[0:1, :]
    fill_row = meta_v[1:2, :]
    pages_t = jnp.broadcast_to(pages_row, (LANES, LANES)).T
    end_row = jnp.sum(jnp.where(sub <= lane, pages_t, 0), axis=0, keepdims=True)
    start_row = end_row - pages_row

    pl.semaphore_wait(bar, n_head - 1 + n_seq - 1)

    for d in HEAD_ORDER:
        k = (h + d) % n_head
        remote(dst_v.at[own], dst_v.at[own], ds, dr, {"head": k}).start()
    load.wait()
    for c in range(CHUNKS):
        for d in HEAD_ORDER:
            k = (h + d) % n_head
            remote(
                old_v.at[:, k, pl.ds(c * TOK, TOK), :], regs[c].at[own], zs.at[c], zr.at[c], {"head": k}
            ).start()
    for c in range(CHUNKS):
        regs[c][own] = old_v[:, h, pl.ds(c * TOK, TOK), :]

    wait_bytes(dst_v.at[pl.ds(0, 56)], dr)
    row, col = iota((64, LANES), 0), iota((64, LANES), 1)
    dest = dst_v[...]
    target, slot = dest >> 6, dest & 63
    chosen = (target == (col >> 2)).astype(jnp.int32)
    count = chosen
    for k in (1, 2, 4, 8, 16, 32):
        count = count + jnp.where(row >= k, pltpu.roll(count, k, 0), 0)
    picked = (chosen > 0) & ((count - chosen) == (col & 3))
    src_row = jnp.sum(jnp.where(picked, row, 0), axis=0, keepdims=True)
    lab_row = jnp.sum(jnp.where(picked, slot + 1, 0), axis=0, keepdims=True) - 1
    lab_out[...] = jnp.broadcast_to(lab_row, (LANES, LANES)).T
    place = slot * n_seq + target
    member = (place >= start_row) & (place < end_row)
    owner = jnp.sum(jnp.where(member, col, 0), axis=1, keepdims=True)
    owner = jnp.broadcast_to(owner, (64, LANES))
    owner_row = jnp.concatenate([owner, owner], axis=0).T[0:1, :]
    last = member & (place == end_row - 1)
    fill = jnp.sum(jnp.where(last, fill_row - LANES, 0), axis=1, keepdims=True) + LANES
    fill_v[...] = jnp.broadcast_to(fill, (64, LANES))
    memb_v[...] = member.astype(jnp.float32)
    tab_v[0:1, :] = jnp.minimum(src_row, 63)
    tab_v[1:2, :] = jnp.minimum(owner_row, 63)
    table = pltpu.make_async_copy(tab_v, tab_s, tsem)
    table.start()
    mine8 = pl.ds(pl.multiple_of(s * 8, 8), 8)
    for o in PEERS:
        t = seq_peer(s, o)
        remote(
            lab_out.at[pl.ds(pl.multiple_of((t // 2) * 8, 8), 8)], lab_in.at[mine8], ls, lr, {"seq": t}
        ).start()
    lab_in[mine8, :] = lab_out[pl.ds(pl.multiple_of((s // 2) * 8, 8), 8), :]
    table.wait()

    def anchors():
        wait_bytes(lab_in.at[pl.ds(0, 248)], lr)
        r, g = iota((256, LANES), 0), iota((256, LANES), 1)
        hit = (lab_in[...] == g) & (((r & 7) >> 2) == s % 2)
        place = jnp.sum(jnp.where(hit, (r >> 3) * 4 + (r & 3), 0), axis=0, keepdims=True)
        tab2_v[0:1, :] = jnp.minimum(place, LANES - 1)
        back = pltpu.make_async_copy(tab2_v, tab2_s, t2sem)
        back.start()
        back.wait()

    def put(c):
        wait_bytes(incs[c].at[pl.ds(0, 124)], xr.at[c])

        @pl.loop(0, 64, unroll=8)
        def _(g):
            out_v[g, pl.ds(c * TOK, TOK), :] = incs[c][tab2_s[0, g]]

    mine4 = pl.ds(s * 4, 4)
    for c in range(CHUNKS):
        wait_bytes(regs[c].at[pl.ds(0, 56)], zr.at[c])

        @pl.loop(0, LANES, unroll=8)
        def _(i):
            outgs[c][i] = regs[c][tab_s[0, i]]

        for o in PEERS:
            t = seq_peer(s, o)
            remote(outgs[c].at[pl.ds(t * 4, 4)], incs[c].at[mine4], xs.at[c], xr.at[c], {"seq": t}).start()
        incs[c][mine4] = outgs[c][mine4]
        if c == 1:
            anchors()
        if c >= 2:
            put(c - 2)

    lane8 = iota((8, LANES), 1)

    def page_rows(p):
        return pl.ds(pl.multiple_of(p * 8, 8), 8)

    def page_kv(p):
        return jnp.concatenate([regs[c][p] for c in range(CHUNKS)], axis=0)

    @pl.loop(0, 64, unroll=8)
    def _(p):
        q = q3[tab_s[1, p]].astype(jnp.bfloat16)
        score = lax.dot_general(
            q, page_kv(p), (((1,), (1,)), ((), ())), preferred_element_type=jnp.float32
        ) * 0.125
        score = jnp.where(lane8 < fill_v[pl.ds(p, 1), :], score, NEG_FILL)
        sc_v[page_rows(p), :] = score

    def seq_max_step(p, best):
        top = jnp.broadcast_to(jnp.max(sc_v[page_rows(p), :], axis=1, keepdims=True), (8, LANES))
        m_v[page_rows(p), :] = top
        return jnp.maximum(best, jnp.where(memb_v[pl.ds(p, 1), :] > 0, top, NEG_FILL))

    best = lax.fori_loop(0, 64, seq_max_step, jnp.full((8, LANES), NEG_FILL, jnp.float32), unroll=8)

    @pl.loop(0, 64, unroll=8)
    def _(p):
        top = m_v[page_rows(p), :]
        weights = jnp.exp(sc_v[page_rows(p), :] - top).astype(jnp.bfloat16)
        total = jnp.sum(weights.astype(jnp.float32), axis=1, keepdims=True)
        summed = lax.dot_general(
            weights, page_kv(p), (((1,), (0,)), ((), ())), preferred_element_type=jnp.float32
        )
        o_v[page_rows(p), :] = jnp.where(lane8 < 64, total, summed)
        c_v[page_rows(p), :] = jnp.where(memb_v[pl.ds(p, 1), :] > 0, jnp.exp(top - best), 0.0)

    best_t = jnp.concatenate([best] * 16, axis=0).T
    lane64 = iota((64, LANES), 1)
    for j in range(8):
        coef = c_v[pl.ds(j, 64, stride=8), :]
        sums = o_v[pl.ds(j, 64, stride=8), :]
        res = lax.dot_general(
            coef.T, sums, (((1,), (0,)), ((), ())),
            precision=lax.Precision.HIGHEST, preferred_element_type=jnp.float32,
        )[0:64, :]
        tops = best_t[0:64, j : j + 1]
        rj_v[j] = jnp.where((lane64 >= 32) & (lane64 < 64), tops, res)
        for b in range(2):
            r4_v[pl.ds(j * 2 + b, 32, stride=16), :] = rj_v[j, pl.ds(b, 32, stride=2), :]

    mine16 = pl.ds(pl.multiple_of(s * 16, 16), 16)
    for o in PEERS:
        t = seq_peer(s, o)
        remote(
            r4_v.at[pl.ds(pl.multiple_of(t * 16, 16), 16)], rb_v.at[mine16], ps, pr, {"seq": t}
        ).start()
    rb_v[mine16, :] = r4_v[mine16, :]

    put(CHUNKS - 2)
    put(CHUNKS - 1)

    wait_bytes(rb_v.at[pl.ds(0, 496)], pr)
    parts = rb_v[...].reshape(n_seq, 16, LANES)
    tops = jnp.broadcast_to(parts[:, :, 32:33], (n_seq, 16, LANES))
    scaled = jnp.exp(tops - jnp.max(tops, axis=0, keepdims=True)) * parts
    acc = jnp.sum(scaled, axis=0)
    att_v[...] = acc / acc[:, 0:1]

    wait_bytes(dst_v.at[pl.ds(0, 56)], ds)
    wait_bytes(lab_in.at[pl.ds(0, 248)], ls)
    wait_bytes(rb_v.at[pl.ds(0, 496)], ps)
    for c in range(CHUNKS):
        wait_bytes(regs[c].at[pl.ds(0, 56)], zs.at[c])
        wait_bytes(incs[c].at[pl.ds(0, 124)], xs.at[c])


def per_device(old_cache, page_dest, seq_pages, last_fill, queries):
    meta = jnp.stack([jnp.pad(seq_pages, (0, 64)), jnp.pad(last_fill, (0, 64))])
    q3 = jnp.pad(queries.reshape(64, 8, 64).astype(jnp.float32), ((0, 0), (0, 0), (0, 64)))
    bf, f32, i32 = jnp.bfloat16, jnp.float32, jnp.int32
    vmem, dma = pltpu.VMEM, pltpu.SemaphoreType.DMA
    new_cache, att = pl.pallas_call(
        kernel,
        out_shape=(
            jax.ShapeDtypeStruct((64, 128, 128), bf),
            jax.ShapeDtypeStruct((16, LANES), f32),
        ),
        in_specs=[
            pl.BlockSpec(memory_space=pl.ANY),
            pl.BlockSpec(memory_space=pltpu.SMEM),
            pl.BlockSpec(memory_space=pltpu.VMEM),
            pl.BlockSpec(memory_space=pltpu.VMEM),
        ],
        out_specs=(pl.BlockSpec(memory_space=pltpu.VMEM), pl.BlockSpec(memory_space=pltpu.VMEM)),
        scratch_shapes=[
            vmem((8, 8, 128, 128), bf),
            vmem((64, LANES), i32),
            vmem((LANES, LANES), i32),
            vmem((256, LANES), i32),
            vmem((8, LANES), i32),
            pltpu.SMEM((8, LANES), i32),
            vmem((8, LANES), i32),
            pltpu.SMEM((8, LANES), i32),
            vmem((64, LANES), i32),
            vmem((64, LANES), f32),
            vmem((512, LANES), f32),
            vmem((512, LANES), f32),
            vmem((512, LANES), f32),
            vmem((512, LANES), f32),
            vmem((8, 64, LANES), f32),
            vmem((512, LANES), f32),
            vmem((512, LANES), f32),
            [vmem((64, TOK, LANES), bf)] * CHUNKS,
            [vmem((128, TOK, LANES), bf)] * CHUNKS,
            [vmem((128, TOK, LANES), bf)] * CHUNKS,
            dma((CHUNKS,)), dma((CHUNKS,)), dma((CHUNKS,)), dma((CHUNKS,)),
            dma, dma, dma, dma, dma, dma, dma, dma, dma,
        ],
        compiler_params=pltpu.CompilerParams(
            collective_id=0, has_side_effects=True, vmem_limit_bytes=40 * 2**20
        ),
    )(old_cache, page_dest, meta, q3)
    attended = att.reshape(8, 2, LANES)[:, :, 64:].transpose(1, 0, 2).reshape(2, 1, 512)
    return new_cache.reshape(64, 1, 128, 128), attended.astype(bf)


def solution(mesh):
    in_specs = (
        P(("seq", "head"), None, None, None),
        P(("seq", "head")),
        P(),
        P(),
        P(None, "head", None),
    )
    out_specs = (P("seq", "head", None, None), P("seq", "head", None))
    return jax.shard_map(
        per_device, mesh=mesh, in_specs=in_specs, out_specs=out_specs, check_vma=False
    )
```

time: 179 us -> 78.9 us (0.44)
  waiting for transfers between devices: 110 us -> 0 us
  Pallas kernels: 0 us -> 72.1 us
  starting transfers between devices: 34.6 us -> 0 us
  local copies, waits for them, and re-layouts: 18.4 us -> 5.96 us
  other arithmetic: 9.7 us -> 0.03 us
  matrix products: 4.63 us -> 0 us
    all_to_all x6 -> x0, waiting for transfers between devices: 110 us -> none  [the longest x1 48.4 us: move_pages(): lax.all_to_all(outgoing, 'seq', split_axis=0, concat_axis=0, tiled=True)]
    pallas_call x0 -> x1, Pallas kernels: none -> 72.1 us  [per_device(): pl.pallas_call(kernel, out_shape=(jax.ShapeDtypeStruct((64, 128, 128), bf...]
    all_to_all x6 -> x0, starting transfers between devices: 34.6 us -> none  [the longest x1 9 us: per_device(): lax.all_to_all(spread, 'head', split_axis=1, concat_axis=0, tiled=True)]
    gather x4 -> x0, local copies, waits for them, and re-layouts: 7.47 us -> none  [the longest x1 3.14 us: move_pages(): return jnp.take(flat_pages, anchor, axis=0)]
    select_n x6 -> x0, other arithmetic: 6.1 us -> none  [the longest x1 3.9 us: route_pages(): jnp.where(filled[:, None, None, None], jnp.take(page_block, source, axis=...]
    dot_general x6 -> x0, matrix products: 4.63 us -> none  [the longest x1 1.94 us: partial_sums(): jnp.einsum('pkgt,pktd->pkgd', weights, page_block[..., head_width:], pref...]
    all_to_all x4 -> x0, local copies, waits for them, and re-layouts: 3.63 us -> none  [the longest x1 2.58 us: per_device(): lax.all_to_all(old_cache, 'head', split_axis=1, concat_axis=0, tiled=True)]
    unnamed x10 -> x5, local copies, waits for them, and re-layouts: 4.04 us -> 3.56 us
  transfers between devices with their start and end apart: 6 -> 0, of which waited for: 6 -> 0; matrix products, arithmetic and copies ran while one was open for 12% -> 0% of each run, Pallas kernels for 0% -> 0%
where the time goes in v1:
time: 78.9 us; the launch traced here: 78.7 us
  Pallas kernels  72.1 us (91%)
  local copies, waits for them, and re-layouts  5.96 us (8%)
    pallas_call x1, Pallas kernels, per_device(): pl.pallas_call(kernel, out_shape=(jax.ShapeDtypeStruct((64, 128, 128), bf...  72.1 us
    unnamed x5, local copies, waits for them, and re-layouts  3.56 us

profile of v1, /device:TPU:1, one launch (start us, length us, event | category | flops | bytes accessed | tf_op | source)
XLA Modules:
  0.0 78.7 jit_solution(11022422642456846011)
XLA Ops:
  0.6 0.7 pad_bitcast_fusion
  1.3 1.0 %convert_element_type.21 = bf16[64,8,64]{2,1,0:T(8,128)(2,1)S(1)} reshape(bf16[64,1,512]{2,0,1:T(8,128)(2,1)} %param.9) | data formatting | bytes 131072 | tf_op jit(solution)/shard_map/convert_element_type | solution.py:241
  2.3 0.0 copy-start
  2.3 1.6 %copy-done = bf16[8,8,128,128]{3,2,1,0:T(8,128)(2,1)S(1)} copy-done((bf16[8,8,128,128]{3,2,1,0:T(8,128)(2,1)S(1)}, bf16[8,8,128,128]{3,2,1,0:T(8,128)(2,1)}, u32[]{:S(2)}) %copy-start) | copy-done | bytes 2097176
  3.9 0.0 copy-start.1
  3.9 0.7 copy-done.1
  4.6 72.1 %shard_map.68 = (bf16[64,128,128]{2,1,0:T(8,128)(2,1)S(1)}, f32[16,128]{1,0:T(8,128)S(1)}) custom-call(bf16[8,8,128,128]{3,2,1,0:T(8,128)(2,1)S(1)} %copy-done, s32[8]{0:T(128)S(1)} %copy-done.1, s32[2,128]{1,0:T(2,128)S(1)} %pad_add_fusion.meta_v, f32[64,8,128]{2,1,0:T(8,128)S(1)} %pad_convert_fusion.q3), custom_call_target="tpu_custom_call" | custom-call | tf_op jit(solution)/shard_map/pallas_call | solution.py:244
  76.7 0.1 slice_bitcast_fusion
  76.7 0.7 convert_element_type.23
  77.4 1.3 %copy.10 = bf16[64,1,128,128]{3,2,1,0:T(8,128)(2,1)} copy(bf16[64,1,128,128]{3,2,1,0:T(8,128)(2,1)S(1)} %bitcast.12) | data formatting | bytes 4194304
  (4 shorter events, 0.0 us)
Async XLA Ops:
  2.3 1.6 %copy-start = (bf16[8,8,128,128]{3,2,1,0:T(8,128)(2,1)S(1)}, bf16[8,8,128,128]{3,2,1,0:T(8,128)(2,1)}, u32[]{:S(2)}) copy-start(bf16[8,8,128,128]{3,2,1,0:T(8,128)(2,1)} %old_hbm.1) | copy-start | bytes 6291460
  3.9 0.7 copy-start.1

commit v2 on v1

v2 whole, which is shorter than its diff:
```python
import functools

import jax
import jax.numpy as jnp
from jax import lax
from jax.experimental import pallas as pl
from jax.experimental.pallas import tpu as pltpu
from jax.sharding import PartitionSpec as P

NEG_FILL = -1e30
CHUNKS = 16
TOK = 8
LAG = 3
LANES = 128
MESH = pl.DeviceIdType.MESH

CHIP_ORDER = (
    (1, 2), (2, 3), (3, 2), (2, 1), (1, 1), (3, 3), (0, 2), (2, 0),
    (1, 3), (3, 1), (2, 2), (0, 1), (1, 0), (0, 3), (3, 0),
)
PEERS = tuple((y, x, c) for c in (0, 1) for y, x in CHIP_ORDER) + ((0, 0, 1),)
HEAD_ORDER = (4, 3, 5, 2, 6, 1, 7)


def iota(shape, dim):
    return lax.broadcasted_iota(jnp.int32, shape, dim)


def seq_peer(seq, offset):
    dy, dx, dc = offset
    y, x, c = seq // 8, (seq // 2) % 4, seq % 2
    return ((y + dy) % 4) * 8 + ((x + dx) % 4) * 2 + (c + dc) % 2


def remote(src, dst, send_sem, recv_sem, device):
    return pltpu.make_async_remote_copy(
        src_ref=src, dst_ref=dst, send_sem=send_sem, recv_sem=recv_sem,
        device_id=device, device_id_type=MESH,
    )


def wait_bytes(ref, sem):
    pltpu.make_async_copy(ref, ref, sem).wait()


def kernel(
    old_hbm, dest_hbm, pages_hbm, fill_hbm, q_hbm, out_v, att_v,
    old_v, q_v, q3, kv_v, dest_s, pages_s, last_s, dst_v, lab_out, lab_in, tab_v, tab_s, tab2_v, tab2_s,
    fill_v, memb_v, m_v, o_v, c_v, rj_v, bt_v, ro_v, rm_v, po_v, pm_v, regs, outgs, incs,
    zs, zr, xs, xr, ds, dr, ls, lr, ps, pr, ms, mr, ld, sd, tsem, t2sem,
):
    h = lax.axis_index("head")
    s = lax.axis_index("seq")
    n_head, n_seq = 8, 32

    small = [
        pltpu.make_async_copy(src, dst, sd.at[i])
        for i, (src, dst) in enumerate(
            ((dest_hbm, dest_s), (pages_hbm, pages_s), (fill_hbm, last_s), (q_hbm, q_v))
        )
    ]
    load = pltpu.make_async_copy(old_hbm, old_v, ld)
    for copy in small:
        copy.start()
    load.start()
    bar = pltpu.get_barrier_semaphore()

    @pl.loop(1, n_head)
    def _(d):
        pl.semaphore_signal(bar, inc=1, device_id={"head": (h + d) % n_head}, device_id_type=MESH)

    @pl.loop(1, n_seq)
    def _(d):
        pl.semaphore_signal(bar, inc=1, device_id={"seq": (s + d) % n_seq}, device_id_type=MESH)

    for copy in small:
        copy.wait()
    own = pl.ds(pl.multiple_of(h * 8, 8), 8)
    row8 = iota((8, LANES), 0)
    mine = jnp.zeros((8, LANES), jnp.int32)
    for i in range(8):
        mine = jnp.where(row8 == i, dest_s[i], mine)
    dst_v[own, :] = mine

    lane1 = iota((1, LANES), 1)
    start_row = jnp.full((1, LANES), 1 << 20, jnp.int32)
    end_row, fill_row = start_row, jnp.zeros((1, LANES), jnp.int32)
    end = jnp.int32(0)
    for k in range(64):
        start_row = jnp.where(lane1 == k, end, start_row)
        end = end + pages_s[k]
        end_row = jnp.where(lane1 == k, end, end_row)
        fill_row = jnp.where(lane1 == k, last_s[k], fill_row)
    lane64 = iota((64, LANES), 1)
    for j in range(8):
        pair = q_v[:, (j // 2) * LANES : (j // 2 + 1) * LANES].astype(jnp.float32)
        if j % 2:
            pair = pltpu.roll(pair, 64, 1)
        q3[:, j, :] = jnp.where(lane64 < 64, pair, 0.0)

    pl.semaphore_wait(bar, n_head - 1 + n_seq - 1)

    for d in HEAD_ORDER:
        k = (h + d) % n_head
        remote(dst_v.at[own], dst_v.at[own], ds, dr, {"head": k}).start()
    load.wait()
    for c in range(CHUNKS):
        for d in HEAD_ORDER:
            k = (h + d) % n_head
            remote(
                old_v.at[:, k, pl.ds(c * TOK, TOK), :], regs[c].at[own], zs.at[c], zr.at[c], {"head": k}
            ).start()
    for c in range(CHUNKS):
        regs[c][own] = old_v[:, h, pl.ds(c * TOK, TOK), :]

    wait_bytes(dst_v.at[pl.ds(0, 56)], dr)
    row, col = iota((64, LANES), 0), iota((64, LANES), 1)
    dest = dst_v[...]
    target, slot = dest >> 6, dest & 63
    chosen = (target == (col >> 2)).astype(jnp.int32)
    count = chosen
    for k in (1, 2, 4, 8, 16, 32):
        count = count + jnp.where(row >= k, pltpu.roll(count, k, 0), 0)
    picked = (chosen > 0) & ((count - chosen) == (col & 3))
    src_row = jnp.sum(jnp.where(picked, row, 0), axis=0, keepdims=True)
    lab_row = jnp.sum(jnp.where(picked, slot + 1, 0), axis=0, keepdims=True) - 1
    lab_out[...] = jnp.broadcast_to(lab_row, (LANES, LANES)).T
    place = slot * n_seq + target
    member = (place >= start_row) & (place < end_row)
    owner = jnp.sum(jnp.where(member, col, 0), axis=1, keepdims=True)
    owner = jnp.broadcast_to(owner, (64, LANES))
    owner_row = jnp.concatenate([owner, owner], axis=0).T[0:1, :]
    last = member & (place == end_row - 1)
    fill = jnp.sum(jnp.where(last, fill_row - LANES, 0), axis=1, keepdims=True) + LANES
    fill_v[...] = jnp.broadcast_to(fill, (64, LANES))
    memb_v[...] = member.astype(jnp.float32)
    tab_v[0:1, :] = jnp.minimum(src_row, 63)
    tab_v[1:2, :] = jnp.minimum(owner_row, 63)
    table = pltpu.make_async_copy(tab_v, tab_s, tsem)
    table.start()
    mine8 = pl.ds(pl.multiple_of(s * 8, 8), 8)
    for o in PEERS:
        t = seq_peer(s, o)
        remote(
            lab_out.at[pl.ds(pl.multiple_of((t // 2) * 8, 8), 8)], lab_in.at[mine8], ls, lr, {"seq": t}
        ).start()
    lab_in[mine8, :] = lab_out[pl.ds(pl.multiple_of((s // 2) * 8, 8), 8), :]
    table.wait()

    def anchors():
        wait_bytes(lab_in.at[pl.ds(0, 248)], lr)
        r, g = iota((256, LANES), 0), iota((256, LANES), 1)
        hit = (lab_in[...] == g) & (((r & 7) >> 2) == s % 2)
        place = jnp.sum(jnp.where(hit, (r >> 3) * 4 + (r & 3), 0), axis=0, keepdims=True)
        tab2_v[0:1, :] = jnp.minimum(place, LANES - 1)
        back = pltpu.make_async_copy(tab2_v, tab2_s, t2sem)
        back.start()
        back.wait()

    def put(c):
        wait_bytes(incs[c].at[pl.ds(0, 124)], xr.at[c])

        @pl.loop(0, 64, unroll=8)
        def _(g):
            out_v[g, pl.ds(c * TOK, TOK), :] = incs[c][tab2_s[0, g]]

    lane8 = iota((8, LANES), 1)
    lane_half = iota((8, 64), 1)

    def page_rows(p):
        return pl.ds(pl.multiple_of(p * 8, 8), 8)

    def attend(half, groups):
        tokens = pl.ds(half * 64, 64)
        for group in groups:
            pages = range(group * 8, group * 8 + 8)
            scores = []
            for p in pages:
                q = q3[tab_s[1, p]].astype(jnp.bfloat16)
                score = lax.dot_general(
                    q, kv_v[p, tokens, :], (((1,), (1,)), ((), ())), preferred_element_type=jnp.float32
                ) * 0.125
                scores.append(jnp.where(lane_half + half * 64 < fill_v[pl.ds(p, 1), 0:64], score, NEG_FILL))
            for p, score in zip(pages, scores):
                top = jnp.max(score, axis=1, keepdims=True)
                weights = jnp.exp(score - top).astype(jnp.bfloat16)
                total = jnp.sum(weights.astype(jnp.float32), axis=1, keepdims=True)
                summed = lax.dot_general(
                    weights, kv_v[p, tokens, :], (((1,), (0,)), ((), ())), preferred_element_type=jnp.float32
                )
                rows = page_rows(half * 64 + p)
                m_v[rows, :] = jnp.broadcast_to(top, (8, LANES))
                o_v[rows, :] = jnp.where(lane8 < 64, total, summed)

    mine4 = pl.ds(s * 4, 4)
    for c in range(CHUNKS):
        wait_bytes(regs[c].at[pl.ds(0, 56)], zr.at[c])

        @pl.loop(0, LANES, unroll=8)
        def _(i):
            outgs[c][i] = regs[c][tab_s[0, i]]

        for o in PEERS:
            t = seq_peer(s, o)
            remote(outgs[c].at[pl.ds(t * 4, 4)], incs[c].at[mine4], xs.at[c], xr.at[c], {"seq": t}).start()
        incs[c][mine4] = outgs[c][mine4]
        kv_v[:, pl.ds(c * TOK, TOK), :] = regs[c][...]
        if c == LAG - 1:
            anchors()
        if c >= LAG:
            put(c - LAG)
        if c >= CHUNKS // 2:
            attend(0, range(c - CHUNKS // 2, c - CHUNKS // 2 + 1))

    attend(1, range(8))
    best = jnp.full((8, LANES), NEG_FILL, jnp.float32)

    def seq_max_step(p, best):
        top = jnp.maximum(m_v[page_rows(p), :], m_v[page_rows(64 + p), :])
        return jnp.maximum(best, jnp.where(memb_v[pl.ds(p, 1), :] > 0, top, NEG_FILL))

    best = lax.fori_loop(0, 64, seq_max_step, best, unroll=16)

    @pl.loop(0, 64, unroll=16)
    def _(p):
        inside = memb_v[pl.ds(p, 1), :] > 0
        for half in range(2):
            rows = page_rows(half * 64 + p)
            c_v[rows, :] = jnp.where(inside, jnp.exp(m_v[rows, :] - best), 0.0)

    bt_v[...] = jnp.concatenate([best] * 16, axis=0).T
    lane32 = iota((32, LANES), 1)
    stats = jnp.zeros((32, LANES), jnp.float32)
    for b in range(2):
        stats = jnp.where(
            (lane32 >> 3) == 2 + b, bt_v[pl.ds(b, 32, stride=2), :], stats
        )
    for j in range(8):
        coef = c_v[pl.ds(j, 128, stride=8), :]
        sums = o_v[pl.ds(j, 128, stride=8), :]
        rj_v[j] = lax.dot_general(
            coef.T, sums, (((1,), (0,)), ((), ())),
            precision=lax.Precision.HIGHEST, preferred_element_type=jnp.float32,
        )[0:64, :]
        even, odd = rj_v[j, pl.ds(0, 32, stride=2), :], rj_v[j, pl.ds(1, 32, stride=2), :]
        stats = jnp.where(lane32 == j, even[:, 0:1], stats)
        stats = jnp.where(lane32 == 8 + j, odd[:, 0:1], stats)
        ro_v[pl.ds(j, 32, stride=8), :] = jnp.where(lane32 < 64, pltpu.roll(even, 64, 1), odd)
    rm_v[:, 0, :] = stats

    for o in PEERS:
        t = seq_peer(s, o)
        remote(
            ro_v.at[pl.ds(pl.multiple_of(t * 8, 8), 8)], po_v.at[mine8], ps, pr, {"seq": t}
        ).start()
        remote(rm_v.at[t], pm_v.at[s], ms, mr, {"seq": t}).start()
    po_v[mine8, :] = ro_v[mine8, :]
    pm_v[s] = rm_v[s]

    for c in range(CHUNKS - LAG, CHUNKS):
        put(c)

    wait_bytes(pm_v.at[pl.ds(0, 31)], mr)
    turned = jnp.concatenate([pm_v[:, 0, :]] * 4, axis=0).T
    totals, tops = turned[0:16, :], turned[16:32, :]
    coef = jnp.exp(tops - jnp.max(tops, axis=1, keepdims=True))
    total = jnp.sum(jnp.where(iota((16, LANES), 1) < n_seq, coef * totals, 0.0), axis=1, keepdims=True)
    coef = coef / total
    wait_bytes(po_v.at[pl.ds(0, 248)], pr)
    acc = jnp.zeros((8, LANES), jnp.float32)
    for t in range(n_seq):
        part = jnp.where(lane8 < 64, coef[0:8, t : t + 1], coef[8:16, t : t + 1])
        acc = acc + part * po_v[t * 8 : (t + 1) * 8, :]
    att_v[...] = acc

    wait_bytes(dst_v.at[pl.ds(0, 56)], ds)
    wait_bytes(lab_in.at[pl.ds(0, 248)], ls)
    wait_bytes(po_v.at[pl.ds(0, 248)], ps)
    wait_bytes(pm_v.at[pl.ds(0, 31)], ms)
    for c in range(CHUNKS):
        wait_bytes(regs[c].at[pl.ds(0, 56)], zs.at[c])
        wait_bytes(incs[c].at[pl.ds(0, 124)], xs.at[c])


def per_device(old_cache, page_dest, seq_pages, last_fill, queries):
    bf, f32, i32 = jnp.bfloat16, jnp.float32, jnp.int32
    vmem, dma = pltpu.VMEM, pltpu.SemaphoreType.DMA
    new_cache, att = pl.pallas_call(
        kernel,
        out_shape=(
            jax.ShapeDtypeStruct((64, 128, 128), bf),
            jax.ShapeDtypeStruct((8, LANES), f32),
        ),
        in_specs=[pl.BlockSpec(memory_space=pltpu.HBM)] * 5,
        out_specs=(pl.BlockSpec(memory_space=pltpu.VMEM), pl.BlockSpec(memory_space=pltpu.VMEM)),
        scratch_shapes=[
            vmem((8, 8, 128, 128), bf),
            vmem((64, 512), bf),
            vmem((64, 8, LANES), f32),
            vmem((64, 128, 128), bf),
            pltpu.SMEM((8,), i32),
            pltpu.SMEM((64,), i32),
            pltpu.SMEM((64,), i32),
            vmem((64, LANES), i32),
            vmem((LANES, LANES), i32),
            vmem((256, LANES), i32),
            vmem((8, LANES), i32),
            pltpu.SMEM((8, LANES), i32),
            vmem((8, LANES), i32),
            pltpu.SMEM((8, LANES), i32),
            vmem((64, LANES), i32),
            vmem((64, LANES), f32),
            vmem((1024, LANES), f32),
            vmem((1024, LANES), f32),
            vmem((1024, LANES), f32),
            vmem((8, 64, LANES), f32),
            vmem((LANES, LANES), f32),
            vmem((256, LANES), f32),
            vmem((32, 1, LANES), f32),
            vmem((256, LANES), f32),
            vmem((32, 1, LANES), f32),
            [vmem((64, TOK, LANES), bf)] * CHUNKS,
            [vmem((128, TOK, LANES), bf)] * CHUNKS,
            [vmem((128, TOK, LANES), bf)] * CHUNKS,
            dma((CHUNKS,)), dma((CHUNKS,)), dma((CHUNKS,)), dma((CHUNKS,)),
            dma, dma, dma, dma, dma, dma, dma, dma, dma, dma((4,)), dma, dma,
        ],
        compiler_params=pltpu.CompilerParams(
            collective_id=0, has_side_effects=True, vmem_limit_bytes=50 * 2**20
        ),
    )(*[pltpu.with_memory_space_constraint(x, pltpu.HBM) for x in (old_cache, page_dest, seq_pages, last_fill, queries.reshape(64, 512))])
    attended = att.reshape(8, 2, 64).transpose(1, 0, 2).reshape(2, 1, 512)
    return new_cache.reshape(64, 1, 128, 128), attended.astype(bf)


def solution(mesh):
    in_specs = (
        P(("seq", "head"), None, None, None),
        P(("seq", "head")),
        P(),
        P(),
        P(None, "head", None),
    )
    out_specs = (P("seq", "head", None, None), P("seq", "head", None))
    return jax.shard_map(
        per_device, mesh=mesh, in_specs=in_specs, out_specs=out_specs, check_vma=False
    )
```

time: 78.9 us -> 72.7 us (0.921)
  local copies, waits for them, and re-layouts: 5.96 us -> 2.07 us
  Pallas kernels: 72.1 us -> 69.9 us
    unnamed x5 -> x1, local copies, waits for them, and re-layouts: 3.56 us -> 1.32 us
    pallas_call x1, Pallas kernels: 72.1 us -> 69.9 us  [per_device(): pl.pallas_call(kernel, out_shape=(jax.ShapeDtypeStruct((64, 128, 128), bf...]
    convert_element_type x1 -> x0, local copies, waits for them, and re-layouts: 0.98 us -> none  [per_device(): queries.reshape(64, 8, 64).astype(jnp.float32)]
where the time goes in v2:
time: 72.7 us; the launch traced here: 72.6 us
  Pallas kernels  69.9 us (96%)
  local copies, waits for them, and re-layouts  2.07 us (3%)
    pallas_call x1, Pallas kernels, per_device(): pl.pallas_call(kernel, out_shape=(jax.ShapeDtypeStruct((64, 128, 128), bf...  69.9 us

profile of v2, /device:TPU:1, one launch (start us, length us, event | category | flops | bytes accessed | tf_op | source)
XLA Modules:
  0.0 72.6 jit_solution(13550840223416669047)
XLA Ops:
  0.6 69.9 %shard_map.68 = (bf16[64,128,128]{2,1,0:T(8,128)(2,1)S(1)}, f32[8,128]{1,0:T(8,128)S(1)}) custom-call(bf16[8,8,128,128]{3,2,1,0:T(8,128)(2,1)} %old_hbm.1, s32[8]{0:T(128)} %dest_hbm.1, s32[64]{0:T(128)} %pages_hbm.1, s32[64]{0:T(128)} %fill_hbm.1, bf16[64,512]{1,0:T(8,128)(2,1)} %bitcast.6), custom_call_target="tpu_custom_call" | custom-call | tf_op jit(solution)/shard_map/pallas_call | solution.py:288
  70.5 0.1 convert_element_type.21
  70.6 0.7 convert_element_type.23
  71.3 1.3 %copy.10 = bf16[64,1,128,128]{3,2,1,0:T(8,128)(2,1)} copy(bf16[64,1,128,128]{3,2,1,0:T(8,128)(2,1)S(1)} %bitcast.5) | data formatting | bytes 4194304
  (2 shorter events, 0.0 us)

commit v3 on v2

--- a/solution.py
+++ b/solution.py
@@ -10,7 +10,7 @@
 NEG_FILL = -1e30
 CHUNKS = 16
 TOK = 8
-LAG = 3
+LAG = 4
 LANES = 128
 MESH = pl.DeviceIdType.MESH
 
@@ -73,8 +73,7 @@
     def _(d):
         pl.semaphore_signal(bar, inc=1, device_id={"seq": (s + d) % n_seq}, device_id_type=MESH)
 
-    for copy in small:
-        copy.wait()
+    small[0].wait()
     own = pl.ds(pl.multiple_of(h * 8, 8), 8)
     row8 = iota((8, LANES), 0)
     mine = jnp.zeros((8, LANES), jnp.int32)
@@ -82,6 +81,23 @@
         mine = jnp.where(row8 == i, dest_s[i], mine)
     dst_v[own, :] = mine
 
+    pl.semaphore_wait(bar, n_head - 1 + n_seq - 1)
+
+    for d in HEAD_ORDER:
+        k = (h + d) % n_head
+        remote(dst_v.at[own], dst_v.at[own], ds, dr, {"head": k}).start()
+    load.wait()
+    for c in range(CHUNKS):
+        for d in HEAD_ORDER:
+            k = (h + d) % n_head
+            remote(
+                old_v.at[:, k, pl.ds(c * TOK, TOK), :], regs[c].at[own], zs.at[c], zr.at[c], {"head": k}
+            ).start()
+    for c in range(CHUNKS):
+        regs[c][own] = old_v[:, h, pl.ds(c * TOK, TOK), :]
+
+    for copy in small[1:]:
+        copy.wait()
     lane1 = iota((1, LANES), 1)
     start_row = jnp.full((1, LANES), 1 << 20, jnp.int32)
     end_row, fill_row = start_row, jnp.zeros((1, LANES), jnp.int32)
@@ -97,21 +113,6 @@
         if j % 2:
             pair = pltpu.roll(pair, 64, 1)
         q3[:, j, :] = jnp.where(lane64 < 64, pair, 0.0)
-
-    pl.semaphore_wait(bar, n_head - 1 + n_seq - 1)
-
-    for d in HEAD_ORDER:
-        k = (h + d) % n_head
-        remote(dst_v.at[own], dst_v.at[own], ds, dr, {"head": k}).start()
-    load.wait()
-    for c in range(CHUNKS):
-        for d in HEAD_ORDER:
-            k = (h + d) % n_head
-            remote(
-                old_v.at[:, k, pl.ds(c * TOK, TOK), :], regs[c].at[own], zs.at[c], zr.at[c], {"head": k}
-            ).start()
-    for c in range(CHUNKS):
-        regs[c][own] = old_v[:, h, pl.ds(c * TOK, TOK), :]
 
     wait_bytes(dst_v.at[pl.ds(0, 56)], dr)
     row, col = iota((64, LANES), 0), iota((64, LANES), 1)
@@ -271,7 +272,13 @@
     for t in range(n_seq):
         part = jnp.where(lane8 < 64, coef[0:8, t : t + 1], coef[8:16, t : t + 1])
         acc = acc + part * po_v[t * 8 : (t + 1) * 8, :]
-    att_v[...] = acc
+    turned = pltpu.roll(acc, 64, 1)
+    low = lane1 < 64
+    for k in range(4):
+        first = jnp.where(low, acc[2 * k : 2 * k + 1], turned[2 * k + 1 : 2 * k + 2])
+        second = jnp.where(low, turned[2 * k : 2 * k + 1], acc[2 * k + 1 : 2 * k + 2])
+        both = jnp.concatenate([first, second], axis=0)
+        att_v[:, k * LANES : (k + 1) * LANES] = both.astype(jnp.bfloat16)
 
     wait_bytes(dst_v.at[pl.ds(0, 56)], ds)
     wait_bytes(lab_in.at[pl.ds(0, 248)], ls)
@@ -282,6 +289,17 @@
         wait_bytes(incs[c].at[pl.ds(0, 124)], xs.at[c])
 
 
+def write_out(cache_v, att_v, cache_hbm, att_hbm, sems):
+    copies = [pltpu.make_async_copy(att_v, att_hbm, sems.at[8])]
+    for i in range(8):
+        pages = pl.ds(i * 8, 8)
+        copies.append(pltpu.make_async_copy(cache_v.at[pages], cache_hbm.at[pages], sems.at[i]))
+    for copy in copies:
+        copy.start()
+    for copy in copies:
+        copy.wait()
+
+
 def per_device(old_cache, page_dest, seq_pages, last_fill, queries):
     bf, f32, i32 = jnp.bfloat16, jnp.float32, jnp.int32
     vmem, dma = pltpu.VMEM, pltpu.SemaphoreType.DMA
@@ -289,7 +307,7 @@
         kernel,
         out_shape=(
             jax.ShapeDtypeStruct((64, 128, 128), bf),
-            jax.ShapeDtypeStruct((8, LANES), f32),
+            jax.ShapeDtypeStruct((2, 512), bf),
         ),
         in_specs=[pl.BlockSpec(memory_space=pltpu.HBM)] * 5,
         out_specs=(pl.BlockSpec(memory_space=pltpu.VMEM), pl.BlockSpec(memory_space=pltpu.VMEM)),
@@ -329,8 +347,18 @@
             collective_id=0, has_side_effects=True, vmem_limit_bytes=50 * 2**20
         ),
     )(*[pltpu.with_memory_space_constraint(x, pltpu.HBM) for x in (old_cache, page_dest, seq_pages, last_fill, queries.reshape(64, 512))])
-    attended = att.reshape(8, 2, 64).transpose(1, 0, 2).reshape(2, 1, 512)
-    return new_cache.reshape(64, 1, 128, 128), attended.astype(bf)
+    new_cache, attended = pl.pallas_call(
+        write_out,
+        out_shape=(
+            jax.ShapeDtypeStruct((64, 128, 128), bf),
+            jax.ShapeDtypeStruct((2, 512), bf),
+        ),
+        in_specs=[pl.BlockSpec(memory_space=pltpu.VMEM)] * 2,
+        out_specs=[pl.BlockSpec(memory_space=pltpu.HBM)] * 2,
+        scratch_shapes=[dma((9,))],
+        compiler_params=pltpu.CompilerParams(vmem_limit_bytes=50 * 2**20),
+    )(new_cache, att)
+    return new_cache.reshape(64, 1, 128, 128), attended.reshape(2, 1, 512)
 
 
 def solution(mesh):

time: 72.7 us -> 71.4 us (0.982)
  local copies, waits for them, and re-layouts: 2.07 us -> 0 us
    pallas_call x0 -> x1, Pallas kernels: none -> 1.39 us  [per_device(): pl.pallas_call(write_out, out_shape=(jax.ShapeDtypeStruct((64, 128, 128),...]
    unnamed x1 -> x0, local copies, waits for them, and re-layouts: 1.32 us -> none
    convert_element_type x3 -> x0, local copies, waits for them, and re-layouts: 0.75 us -> none  [per_device(): return (new_cache.reshape(64, 1, 128, 128), attended.astype(bf))]
where the time goes in v3:
time: 71.4 us; the launch traced here: 71.3 us
  Pallas kernels  70.6 us (99%)
    pallas_call x1, Pallas kernels, per_device(): pl.pallas_call(kernel, out_shape=(jax.ShapeDtypeStruct((64, 128, 128), bf...  69.2 us

profile of v3, /device:TPU:1, one launch (start us, length us, event | category | flops | bytes accessed | tf_op | source)
XLA Modules:
  0.0 71.3 jit_solution(2451724031428265889)
XLA Ops:
  0.6 69.2 %shard_map.68 = (bf16[64,128,128]{2,1,0:T(8,128)(2,1)S(1)}, bf16[2,512]{1,0:T(2,128)(2,1)S(1)}) custom-call(bf16[8,8,128,128]{3,2,1,0:T(8,128)(2,1)} %old_hbm.1, s32[8]{0:T(128)} %dest_hbm.1, s32[64]{0:T(128)} %pages_hbm.1, s32[64]{0:T(128)} %fill_hbm.1, bf16[64,512]{1,0:T(8,128)(2,1)} %bitcast.5), custom_call_target="tpu_custom_call" | custom-call | tf_op jit(solution)/shard_map/pallas_call | solution.py:306
  69.9 1.4 %shard_map.69 = (bf16[64,128,128]{2,1,0:T(8,128)(2,1)}, bf16[2,512]{1,0:T(2,128)(2,1)}) custom-call(bf16[64,128,128]{2,1,0:T(8,128)(2,1)S(1)} %get-tuple-element.6.cache_v, bf16[2,512]{1,0:T(2,128)(2,1)S(1)} %get-tuple-element.7.att_v), custom_call_target="tpu_custom_call" | custom-call | tf_op jit(solution)/shard_map/pallas_call | solution.py:350
